TPU v7x, 32 devices: a whole 2x2x4 slice. The times are simulated.
32 devices in a mesh: seq: 8 (over z, core), head: 4 (over y, x).
Axes of the slice: x: 2, y: 2, z: 4, core: 2. Of those that a mesh axis runs over, the one named last changes fastest.
Arguments:
- queries: bfloat16 [1024, 2048], P('seq', 'head'), may hold values from -192 to 192
- keys: bfloat16 [1024, 512], P('seq', 'head'), may hold values from -5 to 5
- values: bfloat16 [1024, 512], P('seq', 'head'), may hold values from -24 to 24
- segments: int32 [1024], replicated, may hold values from 0 to 5, never falling along the last dimension, each value on 1 to 341 neighbouring positions
- out_weight: bfloat16 [2048, 8192], P(None, 'head'), may hold values from -0.125 to 0.125
Outputs:
- mixed: bfloat16 [1024, 8192], P('seq', 'head')
All inputs are finite; a program needn't handle non-finite values.
Results may differ from a plain program's by a relative error of at most 0.007.
Values may be sent and summed in bfloat16 or wider, within the bound.
A program may use at most 64 MiB of HBM per device.

v0:
```python
import jax
import jax.numpy as jnp
from jax import lax
from jax.sharding import PartitionSpec as P

HD = 128
WIN_BLK = 31


masked_score = -1e30


def passed_along(block, axis, distance):
    devices = range(lax.axis_size(axis))
    route = [(i - distance, i) for i in devices if i - distance in devices]
    return lax.ppermute(block, axis, route)


def allowed_keys(segments, query_pos, query_seg, key_first, key_count, window_len):
    key_pos = key_first + jnp.arange(key_count, dtype=jnp.int32)
    clipped = jnp.clip(key_pos, 0, segments.shape[0] - 1)
    key_seg = jnp.take(segments, clipped)
    allowed = key_pos[None, :] <= query_pos[:, None]
    allowed = allowed & (query_pos[:, None] - key_pos[None, :] < window_len)
    allowed = allowed & (key_pos[None, :] >= 0)
    return allowed & (key_seg[None, :] == query_seg[:, None])


def absorb(carry_state, query_heads, key_piece, value_piece, allowed):
    row_max, row_sum, accum = carry_state
    key_count = key_piece.shape[0]
    kv_heads = query_heads.shape[1]
    key_heads = key_piece.reshape(key_count, kv_heads, HD)
    value_heads = value_piece.reshape(key_count, kv_heads, HD)
    scores = jnp.einsum(
        "tagd,sad->agts", query_heads, key_heads, preferred_element_type=jnp.float32
    )
    scores = jnp.where(allowed[None, None], scores * HD ** (-0.5), masked_score)
    new_max = jnp.maximum(row_max, jnp.max(scores, axis=-1))
    weights = jnp.exp(scores - new_max[..., None])
    factor = jnp.exp(row_max - new_max)
    new_sum = row_sum * factor + jnp.sum(weights, axis=-1)
    update = jnp.einsum(
        "agts,sad->agtd",
        weights.astype(jnp.bfloat16),
        value_heads,
        preferred_element_type=jnp.float32,
    )
    return (new_max, new_sum, accum * factor[..., None] + update)


def on_device(queries, keys, values, segments, out_weight):
    row_count = queries.shape[0]
    kv_width = keys.shape[1]
    kv_heads = kv_width // HD
    group_size = queries.shape[1] // kv_width
    cycle_size = lax.axis_size("seq")
    position = lax.axis_index("seq")
    window_len = WIN_BLK * row_count
    reach_blocks = min(WIN_BLK, cycle_size - 1)
    own_first = position * row_count
    query_pos = own_first + jnp.arange(row_count, dtype=jnp.int32)
    query_seg = lax.dynamic_slice_in_dim(segments, own_first, row_count, 0)
    query_heads = queries.reshape(row_count, kv_heads, group_size, HD)
    start_state = (
        jnp.full((kv_heads, group_size, row_count), masked_score, jnp.float32),
        jnp.zeros((kv_heads, group_size, row_count), jnp.float32),
        jnp.zeros((kv_heads, group_size, row_count, HD), jnp.float32),
    )

    def take_block(carry_state, key_piece, value_piece, key_first):
        allowed = allowed_keys(
            segments, query_pos, query_seg, key_first, key_piece.shape[0], window_len
        )
        return absorb(carry_state, query_heads, key_piece, value_piece, allowed)

    carry_state = take_block(start_state, keys, values, own_first)
    near_keys, near_values = passed_along((keys, values), "seq", 1)
    carry_state = take_block(carry_state, near_keys, near_values, own_first - row_count)
    pair_keys = jnp.concatenate([near_keys, keys], axis=0)
    pair_values = jnp.concatenate([near_values, values], axis=0)

    def pair_turn(turn_index, loop_carry):
        moving_keys, moving_values, inner_state = loop_carry
        moving_keys, moving_values = passed_along((moving_keys, moving_values), "seq", 2)
        key_first = own_first - (2 * turn_index + 3) * row_count
        inner_state = take_block(inner_state, moving_keys, moving_values, key_first)
        return (moving_keys, moving_values, inner_state)

    finished = lax.fori_loop(0, reach_blocks // 2, pair_turn, (pair_keys, pair_values, carry_state))
    carry_state = finished[2]
    row_max, row_sum, accum = carry_state
    attended = (accum / row_sum[..., None]).transpose(2, 0, 1, 3)
    attended = attended.reshape(row_count, queries.shape[1]).astype(jnp.bfloat16)
    mixed = jnp.dot(
        lax.all_gather(attended, "head", axis=1, tiled=True),
        out_weight,
        preferred_element_type=jnp.float32,
    )
    return mixed.astype(jnp.bfloat16)


def solution(mesh):
    return jax.shard_map(
        on_device,
        mesh=mesh,
        in_specs=(P("seq", "head"), P("seq", "head"), P("seq", "head"), P(), P(None, "head")),
        out_specs=P("seq", "head"),
        check_vma=False,
    )
```

profile of v0, /device:TPU:0, one launch (start us, length us, event | category | flops | bytes accessed | tf_op | source)
XLA Modules:
  0.0 60.8 jit_solution(18168356742073294899)
XLA Ops:
  0.0 2.4 %collective-permute-start.2 = (bf16[128,128]{1,0:T(8,128)(2,1)}, bf16[128,128]{1,0:T(8,128)(2,1)S(1)}, u32[]{:S(2)}, u32[]{:S(2)}) collective-permute-start(bf16[128,128]{1,0:T(8,128)(2,1)} %param.10), channel_id=1, source_target_pairs={{0,4},{4,8},{8,12},{12,16},{16,20},{20,24},{24,28},{1,5},{5,9},{9,... | collective-permute-start | bytes 98312 | tf_op jit(solution)/shard_map/ppermute | solution.py:16
  2.4 4.6 %collective-permute-start.3 = (bf16[128,128]{1,0:T(8,128)(2,1)}, bf16[128,128]{1,0:T(8,128)(2,1)S(1)}, u32[]{:S(2)}, u32[]{:S(2)}) collective-permute-start(bf16[128,128]{1,0:T(8,128)(2,1)} %param.11), channel_id=1, source_target_pairs={{0,4},{4,8},{8,12},{12,16},{16,20},{20,24},{24,28},{1,5},{5,9},{9,... | collective-permute-start | bytes 98312 | tf_op jit(solution)/shard_map/ppermute | solution.py:16
  7.1 0.8 %dynamic_slice.3 = s32[128]{0:T(128)S(1)} dynamic-slice(s32[1024]{0:T(1024)} %param.12, s32[]{:T(128)S(6)} %select_n.63), dynamic_slice_sizes={128} | dynamic-slice | bytes 1028 | tf_op jit(solution)/shard_map/dynamic_slice | solution.py:63
  7.8 1.6 %gather_fusion.2 = s32[128]{0:T(128)S(1)} fusion(s32[1024]{0:T(1024)} %param.12, s32[1024]{0:T(1024)S(1)} %pad_clamp_fusion.1), kind=kCustom, calls=%fused_computation.2.clone | custom fusion | bytes 1536 | tf_op jit(solution)/shard_map/jit(_take)/gather | solution.py:22
  9.5 1.6 %gather_fusion.1 = s32[128]{0:T(128)S(1)} fusion(s32[1024]{0:T(1024)} %param.12, s32[1024]{0:T(1024)S(1)} %pad_clamp_fusion.2), kind=kCustom, calls=%fused_computation.clone | custom fusion | bytes 1536 | tf_op jit(solution)/shard_map/jit(_take)/gather | solution.py:22
  11.1 0.2 fusion.40
  11.3 1.1 %fusion.54 = (f32[4,128]{1,0:T(4,128)S(1)}, f32[1,4,128,128]{2,3,1,0:T(8,128)S(1)}) fusion(bf16[128,128]{1,0:T(8,128)(2,1)} %param.10, pred[128,128]{0,1:T(8,128)(4,1)S(1)} %get-tuple-element.284, bf16[128,512]{1,0:T(8,128)(2,1)} %param.9), kind=kOutput, calls=%fused_computation.96 | convolution fusion | flops 16973312 | bytes 444416 | tf_op jit(solution)/shard_map/tagd,sad->agts/dot_general | solution.py:35
  12.4 1.0 %copy.16 = bf16[128,512]{0,1:T(8,128)(2,1)S(1)} copy(bf16[128,512]{1,0:T(8,128)(2,1)} %param.9) | data formatting | bytes 262144 | tf_op args[0]
  13.4 0.1 copy.17
  13.6 0.0 collective-permute-done.2
  13.6 1.1 %fusion.55 = (f32[4,128]{1,0:T(4,128)S(1)}, f32[1,4,128,128]{2,3,1,0:T(8,128)S(1)}) fusion(bf16[128,128]{1,0:T(8,128)(2,1)S(1)} %collective-permute-done.2, pred[128,128]{0,1:T(8,128)(4,1)S(1)} %get-tuple-element.285, bf16[128,512]{1,0:T(8,128)(2,1)} %param.9), kind=kOutput, calls=%fused_computation.97 | convolution fusion | flops 16973312 | bytes 444416 | tf_op jit(solution)/shard_map/tagd,sad->agts/dot_general | solution.py:35
  14.7 0.1 fusion.25
  14.8 1.0 %fusion.19 = f32[4,128,128]{2,1,0:T(8,128)S(1)} fusion(f32[1,4,128,128]{2,3,1,0:T(8,128)S(1)} %get-tuple-element.287, f32[4,128]{1,0:T(4,128)S(1)} %get-tuple-element.278, f32[4,128]{1,0:T(4,128)S(1)} %get-tuple-element.282, f32[4,128]{1,0:T(4,128)S(1)} %get-tuple-element.283, bf16[128,128]{1,0:T(8,128)(2,1)} %param.11), kind=kOutput, calls=%fused_computation.36 | convolution fusion | flops 17039360 | bytes 563200 | tf_op jit(solution)/shard_map/agts,sad->agtd/dot_general | solution.py:43
  15.8 0.1 fusion.27
  15.9 0.8 %pad_maximum_fusion = bf16[256,128]{1,0:T(8,128)(2,1)S(1)} fusion(bf16[128,128]{1,0:T(8,128)(2,1)} %param.10, bf16[128,128]{1,0:T(8,128)(2,1)S(1)} %collective-permute-done.2), kind=kLoop, calls=%fused_computation.58 | loop fusion | flops 131072 | bytes 131072 | tf_op jit(solution)/shard_map/concatenate | solution.py:80
  16.6 0.0 collective-permute-done.3
  16.6 0.8 %pad_maximum_fusion.1 = bf16[256,128]{1,0:T(8,128)(2,1)S(1)} fusion(bf16[128,128]{1,0:T(8,128)(2,1)} %param.11, bf16[128,128]{1,0:T(8,128)(2,1)S(1)} %collective-permute-done.3), kind=kLoop, calls=%fused_computation.59 | loop fusion | flops 131072 | bytes 131072 | tf_op jit(solution)/shard_map/concatenate | solution.py:81
  17.4 0.2 fusion.18
  17.6 26.8 %while.23 = (s32[]{:T(128)}, bf16[256,128]{1,0:T(8,128)(2,1)S(1)}, bf16[256,128]{1,0:T(8,128)(2,1)S(1)}, f32[1,4,128]{2,1,0:T(4,128)S(1)}, f32[1,4,128]{2,1,0:T(...) while((s32[]{:T(128)}, bf16[256,128]{1,0:T(8,128)(2,1)S(1)}, ...), condition=%wide.region_7.9_spmd.clone.clone, body=%wide.region_4.8_spmd.clone.clone.sunk | while | flops 68393600 | bytes 3260693 | solution.py:90
  17.6 3.5 %collective-permute-start = (bf16[256,128]{1,0:T(8,128)(2,1)S(1)}, bf16[256,128]{1,0:T(8,128)(2,1)S(1)}, u32[]{:S(2)}, u32[]{:S(2)}) collective-permute-start(bf16[256,128]{1,0:T(8,128)(2,1)S(1)} %get-tuple-element.384), channel_id=1, source_target_pairs={{0,8},{4,12},{8,16},{12,20},{16,24},{20,28},{1,9},{5,13},{9,17},{1... | collective-permute-start | bytes 196616 | tf_op jit(solution)/shard_map/while/body/eval_jaxpr/ppermute | solution.py:16
  21.1 3.5 %collective-permute-start.1 = (bf16[256,128]{1,0:T(8,128)(2,1)S(1)}, bf16[256,128]{1,0:T(8,128)(2,1)S(1)}, u32[]{:S(2)}, u32[]{:S(2)}) collective-permute-start(bf16[256,128]{1,0:T(8,128)(2,1)S(1)} %get-tuple-element.385), channel_id=1, source_target_pairs={{0,8},{4,12},{8,16},{12,20},{16,24},{20,28},{1,9},{5,13},{9,17},{1... | collective-permute-start | bytes 196616 | tf_op jit(solution)/shard_map/while/body/eval_jaxpr/ppermute | solution.py:16
  24.7 1.9 %gather_fusion = s32[256]{0:T(256)S(1)} fusion(s32[1024]{0:T(1024)} %get-tuple-element.404, s32[1024]{0:T(1024)S(1)} %pad_clamp_fusion.4), kind=kCustom, calls=%fused_computation.1.clone.clone.clone.1 | custom fusion | bytes 3072 | tf_op jit(solution)/shard_map/while/body/eval_jaxpr/jit(_take)/gather | solution.py:22
  26.6 0.2 fusion.71
  26.8 0.0 collective-permute-done
  26.8 0.2 fusion.72
  27.1 0.1 fusion.74
  27.2 0.0 collective-permute-done.1
  27.3 0.3 fusion.75
  27.6 3.5 %collective-permute-start = (bf16[256,128]{1,0:T(8,128)(2,1)S(1)}, bf16[256,128]{1,0:T(8,128)(2,1)S(1)}, u32[]{:S(2)}, u32[]{:S(2)}) collective-permute-start(bf16[256,128]{1,0:T(8,128)(2,1)S(1)} %get-tuple-element.384), channel_id=1, source_target_pairs={{0,8},{4,12},{8,16},{12,20},{16,24},{20,28},{1,9},{5,13},{9,17},{1... | collective-permute-start | bytes 196616 | tf_op jit(solution)/shard_map/while/body/eval_jaxpr/ppermute | solution.py:16
  31.1 1.9 %collective-permute-start.1 = (bf16[256,128]{1,0:T(8,128)(2,1)S(1)}, bf16[256,128]{1,0:T(8,128)(2,1)S(1)}, u32[]{:S(2)}, u32[]{:S(2)}) collective-permute-start(bf16[256,128]{1,0:T(8,128)(2,1)S(1)} %get-tuple-element.385), channel_id=1, source_target_pairs={{0,8},{4,12},{8,16},{12,20},{16,24},{20,28},{1,9},{5,13},{9,17},{1... | collective-permute-start | bytes 196616 | tf_op jit(solution)/shard_map/while/body/eval_jaxpr/ppermute | solution.py:16
  33.1 1.9 %gather_fusion = s32[256]{0:T(256)S(1)} fusion(s32[1024]{0:T(1024)} %get-tuple-element.404, s32[1024]{0:T(1024)S(1)} %pad_clamp_fusion.4), kind=kCustom, calls=%fused_computation.1.clone.clone.clone.1 | custom fusion | bytes 3072 | tf_op jit(solution)/shard_map/while/body/eval_jaxpr/jit(_take)/gather | solution.py:22
  35.1 0.2 fusion.71
  35.3 0.0 collective-permute-done
  35.3 0.2 fusion.72
  35.5 0.1 fusion.74
  35.7 0.0 collective-permute-done.1
  35.7 0.3 fusion.75
  36.0 3.5 %collective-permute-start = (bf16[256,128]{1,0:T(8,128)(2,1)S(1)}, bf16[256,128]{1,0:T(8,128)(2,1)S(1)}, u32[]{:S(2)}, u32[]{:S(2)}) collective-permute-start(bf16[256,128]{1,0:T(8,128)(2,1)S(1)} %get-tuple-element.384), channel_id=1, source_target_pairs={{0,8},{4,12},{8,16},{12,20},{16,24},{20,28},{1,9},{5,13},{9,17},{1... | collective-permute-start | bytes 196616 | tf_op jit(solution)/shard_map/while/body/eval_jaxpr/ppermute | solution.py:16
  39.6 1.9 %collective-permute-start.1 = (bf16[256,128]{1,0:T(8,128)(2,1)S(1)}, bf16[256,128]{1,0:T(8,128)(2,1)S(1)}, u32[]{:S(2)}, u32[]{:S(2)}) collective-permute-start(bf16[256,128]{1,0:T(8,128)(2,1)S(1)} %get-tuple-element.385), channel_id=1, source_target_pairs={{0,8},{4,12},{8,16},{12,20},{16,24},{20,28},{1,9},{5,13},{9,17},{1... | collective-permute-start | bytes 196616 | tf_op jit(solution)/shard_map/while/body/eval_jaxpr/ppermute | solution.py:16
  41.6 1.9 %gather_fusion = s32[256]{0:T(256)S(1)} fusion(s32[1024]{0:T(1024)} %get-tuple-element.404, s32[1024]{0:T(1024)S(1)} %pad_clamp_fusion.4), kind=kCustom, calls=%fused_computation.1.clone.clone.clone.1 | custom fusion | bytes 3072 | tf_op jit(solution)/shard_map/while/body/eval_jaxpr/jit(_take)/gather | solution.py:22
  43.5 0.2 fusion.71
  43.7 0.0 collective-permute-done
  43.7 0.2 fusion.72
  44.0 0.1 fusion.74
  44.1 0.0 collective-permute-done.1
  44.1 0.3 fusion.75
  44.5 0.1 copy.18
  44.7 10.7 %all_gather.3 = bf16[128,2048]{0,1:T(8,128)(2,1)S(1)} all-gather(bf16[128,512]{0,1:T(8,128)(2,1)S(1)} %bitcast.142), channel_id=1, replica_groups=mesh['seq'=8,'head'=4] {'head'}, dimensions={1}, use_global_device_ids=true | all-gather | bytes 655360 | tf_op jit(solution)/shard_map/all_gather | solution.py:96
  55.3 5.5 %convolution_convert_fusion = bf16[128,2048]{1,0:T(8,128)(2,1)} fusion(bf16[128,2048]{0,1:T(8,128)(2,1)S(1)} %all_gather.3, bf16[2048,2048]{1,0:T(8,128)(2,1)} %param.13), kind=kOutput, calls=%fused_computation.32 | convolution fusion | flops 1074003968 | bytes 9437184 | tf_op jit(solution)/shard_map/dot_general | solution.py:95
  (40 shorter events, 0.3 us)
Async XLA Ops:
  0.0 13.6 %collective-permute-start.2 = (bf16[128,128]{1,0:T(8,128)(2,1)}, bf16[128,128]{1,0:T(8,128)(2,1)S(1)}, u32[]{:S(2)}, u32[]{:S(2)}) collective-permute-start(bf16[128,128]{1,0:T(8,128)(2,1)} %param.10), channel_id=1, source_target_pairs={{0,4},{4,8},{8,12},{12,16},{16,20},{20,24},{24,28},{1,5},{5,9},{9,... | collective-permute-start | bytes 98312 | tf_op jit(solution)/shard_map/ppermute | solution.py:16
  2.4 14.2 %collective-permute-start.3 = (bf16[128,128]{1,0:T(8,128)(2,1)}, bf16[128,128]{1,0:T(8,128)(2,1)S(1)}, u32[]{:S(2)}, u32[]{:S(2)}) collective-permute-start(bf16[128,128]{1,0:T(8,128)(2,1)} %param.11), channel_id=1, source_target_pairs={{0,4},{4,8},{8,12},{12,16},{16,20},{20,24},{24,28},{1,5},{5,9},{9,... | collective-permute-start | bytes 98312 | tf_op jit(solution)/shard_map/ppermute | solution.py:16
  17.6 9.2 %collective-permute-start = (bf16[256,128]{1,0:T(8,128)(2,1)S(1)}, bf16[256,128]{1,0:T(8,128)(2,1)S(1)}, u32[]{:S(2)}, u32[]{:S(2)}) collective-permute-start(bf16[256,128]{1,0:T(8,128)(2,1)S(1)} %get-tuple-element.384), channel_id=1, source_target_pairs={{0,8},{4,12},{8,16},{12,20},{16,24},{20,28},{1,9},{5,13},{9,17},{1... | collective-permute-start | bytes 196616 | tf_op jit(solution)/shard_map/while/body/eval_jaxpr/ppermute | solution.py:16
  21.1 6.1 %collective-permute-start.1 = (bf16[256,128]{1,0:T(8,128)(2,1)S(1)}, bf16[256,128]{1,0:T(8,128)(2,1)S(1)}, u32[]{:S(2)}, u32[]{:S(2)}) collective-permute-start(bf16[256,128]{1,0:T(8,128)(2,1)S(1)} %get-tuple-element.385), channel_id=1, source_target_pairs={{0,8},{4,12},{8,16},{12,20},{16,24},{20,28},{1,9},{5,13},{9,17},{1... | collective-permute-start | bytes 196616 | tf_op jit(solution)/shard_map/while/body/eval_jaxpr/ppermute | solution.py:16
  27.6 7.7 %collective-permute-start = (bf16[256,128]{1,0:T(8,128)(2,1)S(1)}, bf16[256,128]{1,0:T(8,128)(2,1)S(1)}, u32[]{:S(2)}, u32[]{:S(2)}) collective-permute-start(bf16[256,128]{1,0:T(8,128)(2,1)S(1)} %get-tuple-element.384), channel_id=1, source_target_pairs={{0,8},{4,12},{8,16},{12,20},{16,24},{20,28},{1,9},{5,13},{9,17},{1... | collective-permute-start | bytes 196616 | tf_op jit(solution)/shard_map/while/body/eval_jaxpr/ppermute | solution.py:16
  31.1 4.5 %collective-permute-start.1 = (bf16[256,128]{1,0:T(8,128)(2,1)S(1)}, bf16[256,128]{1,0:T(8,128)(2,1)S(1)}, u32[]{:S(2)}, u32[]{:S(2)}) collective-permute-start(bf16[256,128]{1,0:T(8,128)(2,1)S(1)} %get-tuple-element.385), channel_id=1, source_target_pairs={{0,8},{4,12},{8,16},{12,20},{16,24},{20,28},{1,9},{5,13},{9,17},{1... | collective-permute-start | bytes 196616 | tf_op jit(solution)/shard_map/while/body/eval_jaxpr/ppermute | solution.py:16
  36.0 7.7 %collective-permute-start = (bf16[256,128]{1,0:T(8,128)(2,1)S(1)}, bf16[256,128]{1,0:T(8,128)(2,1)S(1)}, u32[]{:S(2)}, u32[]{:S(2)}) collective-permute-start(bf16[256,128]{1,0:T(8,128)(2,1)S(1)} %get-tuple-element.384), channel_id=1, source_target_pairs={{0,8},{4,12},{8,16},{12,20},{16,24},{20,28},{1,9},{5,13},{9,17},{1... | collective-permute-start | bytes 196616 | tf_op jit(solution)/shard_map/while/body/eval_jaxpr/ppermute | solution.py:16
  39.6 4.6 %collective-permute-start.1 = (bf16[256,128]{1,0:T(8,128)(2,1)S(1)}, bf16[256,128]{1,0:T(8,128)(2,1)S(1)}, u32[]{:S(2)}, u32[]{:S(2)}) collective-permute-start(bf16[256,128]{1,0:T(8,128)(2,1)S(1)} %get-tuple-element.385), channel_id=1, source_target_pairs={{0,8},{4,12},{8,16},{12,20},{16,24},{20,28},{1,9},{5,13},{9,17},{1... | collective-permute-start | bytes 196616 | tf_op jit(solution)/shard_map/while/body/eval_jaxpr/ppermute | solution.py:16
where the time goes:
time: 61.6 us; the launch traced here: 60.8 us
  starting transfers between devices  24.9 us (40%)
  local copies, waits for them, and re-layouts  11.1 us (18%)
  blocking collectives  10.7 us (17%)
  matrix products  10.6 us (17%)
  other arithmetic  2.91 us (5%)
    ppermute x8, starting transfers between devices, passed_along(): return lax.ppermute(block, axis, route)  24.9 us
    all_gather x1, blocking collectives, on_device(): lax.all_gather(attended, 'head', axis=1, tiled=True)  10.7 us
    gather x5, local copies, waits for them, and re-layouts, allowed_keys(): key_seg = jnp.take(segments, clipped)  9.02 us
    dot_general x1, matrix products, on_device(): jnp.dot(lax.all_gather(attended, 'head', axis=1, tiled=True), out_weight,...  5.47 us
    dot_general x5, matrix products, absorb(): jnp.einsum('tagd,sad->agts', query_heads, key_heads, preferred_element_ty...  2.97 us
    dot_general x5, matrix products, absorb(): jnp.einsum('agts,sad->agtd', weights.astype(jnp.bfloat16), value_heads, p...  2.2 us
  transfers between devices with their start and end apart: 8, of which 0 were waited for; matrix products, arithmetic and copies ran while one was open for 28% of the time, Pallas kernels for 0%

commit v1 on v0

--- a/solution.py
+++ b/solution.py
@@ -1,6 +1,11 @@
+import functools
+import math
+
 import jax
 import jax.numpy as jnp
 from jax import lax
+from jax.experimental import pallas as pl
+from jax.experimental.pallas import tpu as pltpu
 from jax.sharding import PartitionSpec as P
 
 HD = 128
@@ -100,9 +105,207 @@
     return mixed.astype(jnp.bfloat16)
 
 
+SUBTILE = 16
+MAX_REACH = 3
+PAIRS = 2
+
+
+def needed_reach(token_count, row_count, cycle_size):
+    back = token_count // 3 - 1
+    return min(WIN_BLK, cycle_size - 1, -(-back // row_count))
+
+
+def fused_kernel(
+    reach, far_rows, cycle_size, q_hbm, k_hbm, v_hbm, seg_hbm, w_hbm, out_ref,
+    q_ref, kv_ref, seg_ref, w_ref, att_ref, acc_ref,
+    load_sem, w_sem, kv_send, kv_recv, att_send, att_recv,
+):
+    rows = k_hbm.shape[0]
+    width = q_hbm.shape[1]
+    group = width // HD
+    pair_width = width // PAIRS
+    seq = lax.axis_index("seq")
+    head = lax.axis_index("head")
+    x_at, y_at = head % 2, head // 2
+    peers = (head, head + 1 - 2 * x_at, head + 2 - 4 * y_at, 3 - head)
+    own_at = reach * rows
+
+    barrier = pltpu.get_barrier_semaphore()
+    for peer in peers[1:]:
+        pl.semaphore_signal(barrier, inc=1, device_id={"head": peer})
+    for d in range(1, reach + 1):
+        @pl.when(seq + d < cycle_size)
+        def _():
+            pl.semaphore_signal(barrier, inc=1, device_id={"seq": seq + d})
+
+        @pl.when(seq - d >= 0)
+        def _():
+            pl.semaphore_signal(barrier, inc=1, device_id={"seq": seq - d})
+
+    own = [
+        pltpu.make_async_copy(src, kv_ref.at[i, pl.ds(own_at, rows), :], load_sem.at[i])
+        for i, src in enumerate((k_hbm, v_hbm))
+    ]
+    q_load = pltpu.make_async_copy(q_hbm, q_ref, load_sem.at[2])
+    seg_load = pltpu.make_async_copy(seg_hbm, seg_ref, load_sem.at[3])
+    for copy in own + [q_load, seg_load]:
+        copy.start()
+    w_loads = []
+    for r, peer in enumerate(peers):
+        first = pl.multiple_of(peer * width, width)
+        w_loads.append(pltpu.make_async_copy(w_hbm.at[pl.ds(first, width), :], w_ref.at[r], w_sem.at[r]))
+        w_loads[r].start()
+
+    def kv_copy(d, i):
+        skip = rows - far_rows if d == reach else 0
+        return pltpu.make_async_remote_copy(
+            src_ref=kv_ref.at[i, pl.ds(own_at + skip, rows - skip), :],
+            dst_ref=kv_ref.at[i, pl.ds(own_at - d * rows + skip, rows - skip), :],
+            send_sem=kv_send.at[d - 1, i],
+            recv_sem=kv_recv.at[d - 1, i],
+            device_id={"seq": seq + d},
+        )
+
+    if far_rows < rows:
+        kv_ref[:, : rows - far_rows, :] = jnp.zeros((2, rows - far_rows, HD), jnp.bfloat16)
+    for d in range(1, reach + 1):
+        skip = rows - far_rows if d == reach else 0
+
+        @pl.when(seq - d < 0)
+        def _():
+            kv_ref[:, pl.ds(own_at - d * rows + skip, rows - skip), :] = jnp.zeros(
+                (2, rows - skip, HD), jnp.bfloat16)
+
+    greeted = 3 + jnp.minimum(seq, reach) + jnp.minimum(cycle_size - 1 - seq, reach)
+    pl.semaphore_wait(barrier, greeted)
+
+    for i in range(2):
+        own[i].wait()
+        for d in range(reach, 0, -1):
+            @pl.when(seq + d < cycle_size)
+            def _():
+                kv_copy(d, i).start()
+
+    seg_load.wait()
+    length = (reach + 1) * rows
+    key_seg = jnp.concatenate(
+        [seg_ref[pl.ds((seq - d + cycle_size) % cycle_size, 1), :] for d in range(reach, -1, -1)], axis=1)
+    seg_own = seg_ref[pl.ds(seq, 1), :]
+    query_seg = jnp.broadcast_to(seg_own, (rows, rows)).T
+    query_seg = jnp.concatenate([query_seg] * (reach + 1), axis=1)
+    query_pos = seq * rows + lax.broadcasted_iota(jnp.int32, (rows, length), 0)
+    key_pos = (seq - reach) * rows + lax.broadcasted_iota(jnp.int32, (rows, length), 1)
+    allowed = (key_pos <= query_pos) & (query_pos - key_pos < WIN_BLK * rows) & (key_pos >= 0)
+    allowed = allowed & (key_seg == query_seg)
+
+    q_load.wait()
+
+    def arrivals(i):
+        for d in range(1, reach + 1):
+            @pl.when(seq - d >= 0)
+            def _():
+                kv_copy(d, i).wait_recv()
+
+    arrivals(0)
+    arrivals(1)
+    factor = HD ** (-0.5) * math.log2(math.e)
+
+    def att_copy(r, c):
+        return pltpu.make_async_remote_copy(
+            src_ref=att_ref.at[0, c],
+            dst_ref=att_ref.at[r, c],
+            send_sem=att_send.at[r - 1, c],
+            recv_sem=att_recv.at[r - 1, c],
+            device_id={"head": peers[r]},
+        )
+
+    per_pair = group // PAIRS
+    for h in range(group):
+        q_h = q_ref[:, h * HD:(h + 1) * HD]
+        scores = lax.dot_general(
+            q_h, kv_ref[0], (((1,), (1,)), ((), ())), preferred_element_type=jnp.float32)
+        scores = jnp.where(allowed, scores, masked_score)
+        row_max = jnp.max(scores, axis=1, keepdims=True)
+        raw = jnp.exp2((scores - row_max) * factor)
+        total = jnp.sum(raw, axis=1, keepdims=True)
+        part = jnp.dot(raw.astype(jnp.bfloat16), kv_ref[1], preferred_element_type=jnp.float32)
+        c, place = h // per_pair, h % per_pair
+        att_ref[0, c, :, place * HD:(place + 1) * HD] = (part / total).astype(jnp.bfloat16)
+        if place == per_pair - 1:
+            for r in (3, 1, 2):
+                att_copy(r, c).start()
+
+    order = [(0, 0), (0, 1)] + [(r, c) for c in range(PAIRS) for r in (1, 2, 3)]
+    for step, (r, c) in enumerate(order):
+        if r:
+            att_copy(r, c).wait_recv()
+        if c == 0:
+            w_loads[r].wait()
+        piece = jnp.dot(
+            att_ref[r, c], w_ref[r, c * pair_width:(c + 1) * pair_width, :],
+            preferred_element_type=jnp.float32)
+        if step == 0:
+            acc_ref[...] = piece
+        elif step < len(order) - 1:
+            acc_ref[...] += piece
+        else:
+            out_ref[...] = (acc_ref[...] + piece).astype(jnp.bfloat16)
+
+    for d in range(1, reach + 1):
+        @pl.when(seq + d < cycle_size)
+        def _():
+            kv_copy(d, 0).wait_send()
+            kv_copy(d, 1).wait_send()
+    for r in range(1, 4):
+        for c in range(PAIRS):
+            att_copy(r, c).wait_send()
+
+
+def fused(reach, queries, keys, values, segments, out_weight):
+    rows, width = queries.shape
+    cycle_size = lax.axis_size("seq")
+    features = out_weight.shape[1]
+    back = segments.shape[0] // 3 - 1 - (reach - 1) * rows
+    far_rows = min(rows, -(-back // SUBTILE) * SUBTILE)
+    any_spec = pl.BlockSpec(memory_space=pl.ANY)
+    pair_width = width // PAIRS
+    return pl.pallas_call(
+        functools.partial(fused_kernel, reach, far_rows, cycle_size),
+        out_shape=jax.ShapeDtypeStruct((rows, features), jnp.bfloat16),
+        in_specs=[any_spec] * 5,
+        out_specs=pl.BlockSpec(memory_space=pltpu.VMEM),
+        scratch_shapes=[
+            pltpu.VMEM((rows, width), jnp.bfloat16),
+            pltpu.VMEM((2, (reach + 1) * rows, HD), jnp.bfloat16),
+            pltpu.VMEM((cycle_size, rows), jnp.int32),
+            pltpu.VMEM((4, width, features), jnp.bfloat16),
+            pltpu.VMEM((4, PAIRS, rows, pair_width), jnp.bfloat16),
+            pltpu.VMEM((rows, features), jnp.float32),
+            pltpu.SemaphoreType.DMA((4,)),
+            pltpu.SemaphoreType.DMA((4,)),
+            pltpu.SemaphoreType.DMA((reach, 2)),
+            pltpu.SemaphoreType.DMA((reach, 2)),
+            pltpu.SemaphoreType.DMA((3, PAIRS)),
+            pltpu.SemaphoreType.DMA((3, PAIRS)),
+        ],
+        compiler_params=pltpu.CompilerParams(collective_id=0, has_side_effects=True),
+    )(queries, keys, values, segments.reshape(cycle_size, rows), out_weight)
+
+
+def chosen(queries, keys, values, segments, out_weight):
+    row_count, width = queries.shape
+    cycle_size = lax.axis_size("seq")
+    reach = needed_reach(segments.shape[0], row_count, cycle_size)
+    fits = 1 <= reach <= MAX_REACH and lax.axis_size("head") == 4
+    fits = fits and keys.shape[1] == HD and width % (PAIRS * HD) == 0
+    if fits and row_count == HD and 4 * width == out_weight.shape[0]:
+        return fused(reach, queries, keys, values, segments, out_weight)
+    return on_device(queries, keys, values, segments, out_weight)
+
+
 def solution(mesh):
     return jax.shard_map(
-        on_device,
+        chosen,
         mesh=mesh,
         in_specs=(P("seq", "head"), P("seq", "head"), P("seq", "head"), P(), P(None, "head")),
         out_specs=P("seq", "head"),

time: 61.6 us -> 19.2 us (0.31)
  the two profiles are of different devices: /device:TPU:0 before, /device:TPU:16 now
where the time goes in v1:
time: 19.2 us; the launch traced here: 19 us
  Pallas kernels  17.2 us (90%)
  local copies, waits for them, and re-layouts  1.88 us (10%)
    pallas_call x1, Pallas kernels, fused(): pl.pallas_call(functools.partial(fused_kernel, reach, far_rows, cycle_siz...  17.2 us
    unnamed x1, local copies, waits for them, and re-layouts  1.88 us

profile of v1, /device:TPU:16, one launch (start us, length us, event | category | flops | bytes accessed | tf_op | source)
XLA Modules:
  0.0 19.0 jit_solution(12692299656687889448)
XLA Ops:
  0.0 17.2 %shard_map.55 = bf16[128,2048]{1,0:T(8,128)(2,1)} custom-call(bf16[128,512]{1,0:T(8,128)(2,1)} %q_hbm.1, bf16[128,128]{1,0:T(8,128)(2,1)} %k_hbm.1, bf16[128,128]{1,0:T(8,128)(2,1)} %v_hbm.1, s32[8,128]{1,0:T(8,128)} %bitcast.1, bf16[2048,2048]{1,0:T(8,128)(2,1)} %w_hbm.1), custom_call_target="tpu_custom_call" | custom-call | tf_op jit(solution)/shard_map/pallas_call | solution.py:272
  17.2 1.9 %copy.7 = bf16[128,2048]{1,0:T(8,128)(2,1)} copy(bf16[128,2048]{1,0:T(8,128)(2,1)} %shard_map.55) | data formatting | bytes 1048576

commit v2 on v1

--- a/solution.py
+++ b/solution.py
@@ -108,6 +108,7 @@
 SUBTILE = 16
 MAX_REACH = 3
 PAIRS = 2
+VMEM_GRANT = 32 * 2**20
 
 
 def needed_reach(token_count, row_count, cycle_size):
@@ -267,12 +268,13 @@
     features = out_weight.shape[1]
     back = segments.shape[0] // 3 - 1 - (reach - 1) * rows
     far_rows = min(rows, -(-back // SUBTILE) * SUBTILE)
-    any_spec = pl.BlockSpec(memory_space=pl.ANY)
+    hbm_spec = pl.BlockSpec(memory_space=pltpu.HBM)
     pair_width = width // PAIRS
+    operands = (queries, keys, values, segments.reshape(cycle_size, rows), out_weight)
     return pl.pallas_call(
         functools.partial(fused_kernel, reach, far_rows, cycle_size),
-        out_shape=jax.ShapeDtypeStruct((rows, features), jnp.bfloat16),
-        in_specs=[any_spec] * 5,
+        out_shape=pltpu.VMEM((rows, features), jnp.bfloat16),
+        in_specs=[hbm_spec] * 5,
         out_specs=pl.BlockSpec(memory_space=pltpu.VMEM),
         scratch_shapes=[
             pltpu.VMEM((rows, width), jnp.bfloat16),
@@ -288,8 +290,9 @@
             pltpu.SemaphoreType.DMA((3, PAIRS)),
             pltpu.SemaphoreType.DMA((3, PAIRS)),
         ],
-        compiler_params=pltpu.CompilerParams(collective_id=0, has_side_effects=True),
-    )(queries, keys, values, segments.reshape(cycle_size, rows), out_weight)
+        compiler_params=pltpu.CompilerParams(
+            collective_id=0, has_side_effects=True, vmem_limit_bytes=VMEM_GRANT),
+    )(*(pltpu.with_memory_space_constraint(a, pltpu.HBM) for a in operands))
 
 
 def chosen(queries, keys, values, segments, out_weight):

time: 19.2 us -> 17.3 us (0.901)
  local copies, waits for them, and re-layouts: 1.88 us -> 0.8 us
  Pallas kernels: 17.2 us -> 16.4 us
    unnamed x1, local copies, waits for them, and re-layouts: 1.88 us -> 0.8 us
    pallas_call x1, Pallas kernels: 17.2 us -> 16.4 us  [fused(): pl.pallas_call(functools.partial(fused_kernel, reach, far_rows, cycle_siz...]
where the time goes in v2:
time: 17.3 us; the launch traced here: 17.2 us
  Pallas kernels  16.4 us (95%)
  local copies, waits for them, and re-layouts  0.8 us (5%)
    pallas_call x1, Pallas kernels, fused(): pl.pallas_call(functools.partial(fused_kernel, reach, far_rows, cycle_siz...  16.4 us
    unnamed x1, local copies, waits for them, and re-layouts  0.8 us

profile of v2, /device:TPU:16, one launch (start us, length us, event | category | flops | bytes accessed | tf_op | source)
XLA Modules:
  0.0 17.2 jit_solution(15048798500076656978)
XLA Ops:
  0.0 16.4 %shard_map.55 = bf16[128,2048]{1,0:T(8,128)(2,1)S(1)} custom-call(bf16[128,512]{1,0:T(8,128)(2,1)} %q_hbm.1, bf16[128,128]{1,0:T(8,128)(2,1)} %k_hbm.1, bf16[128,128]{1,0:T(8,128)(2,1)} %v_hbm.1, s32[8,128]{1,0:T(8,128)} %bitcast.1, bf16[2048,2048]{1,0:T(8,128)(2,1)} %w_hbm.1), custom_call_target="tpu_custom_call" | custom-call | tf_op jit(solution)/shard_map/pallas_call | solution.py:274
  16.4 0.8 %copy.7 = bf16[128,2048]{1,0:T(8,128)(2,1)} copy(bf16[128,2048]{1,0:T(8,128)(2,1)S(1)} %shard_map.55) | data formatting | bytes 1048576

commit v3 on v2

--- a/solution.py
+++ b/solution.py
@@ -106,7 +106,7 @@
 
 
 SUBTILE = 16
-MAX_REACH = 3
+REACH = 3
 PAIRS = 2
 VMEM_GRANT = 32 * 2**20
 
@@ -131,17 +131,24 @@
     peers = (head, head + 1 - 2 * x_at, head + 2 - 4 * y_at, 3 - head)
     own_at = reach * rows
 
+    core = seq % 2
+    partner = seq + 1 - 2 * core
+    has_next, has_last = seq + 2 < cycle_size, seq - 2 >= 0
+    sends_far = (core == 1) & (seq + 3 < cycle_size)
+    takes_far = (core == 0) & (seq - 3 >= 0)
+
     barrier = pltpu.get_barrier_semaphore()
-    for peer in peers[1:]:
-        pl.semaphore_signal(barrier, inc=1, device_id={"head": peer})
-    for d in range(1, reach + 1):
-        @pl.when(seq + d < cycle_size)
-        def _():
-            pl.semaphore_signal(barrier, inc=1, device_id={"seq": seq + d})
-
-        @pl.when(seq - d >= 0)
-        def _():
-            pl.semaphore_signal(barrier, inc=1, device_id={"seq": seq - d})
+
+    def greet(axis, place):
+        pl.semaphore_signal(barrier, inc=1, device_id={axis: place})
+
+    pl.when(has_next)(lambda: greet("seq", seq + 2))
+    pl.when(has_last)(lambda: greet("seq", seq - 2))
+    pl.when(sends_far)(lambda: greet("seq", seq + 3))
+    pl.when(takes_far)(lambda: greet("seq", seq - 3))
+    greet("head", peers[1])
+    greet("head", peers[2])
+    greet("seq", partner)
 
     own = [
         pltpu.make_async_copy(src, kv_ref.at[i, pl.ds(own_at, rows), :], load_sem.at[i])
@@ -157,14 +164,14 @@
         w_loads.append(pltpu.make_async_copy(w_hbm.at[pl.ds(first, width), :], w_ref.at[r], w_sem.at[r]))
         w_loads[r].start()
 
-    def kv_copy(d, i):
+    def kv_copy(held, d, i, target):
         skip = rows - far_rows if d == reach else 0
         return pltpu.make_async_remote_copy(
-            src_ref=kv_ref.at[i, pl.ds(own_at + skip, rows - skip), :],
+            src_ref=kv_ref.at[i, pl.ds(own_at - held * rows + skip, rows - skip), :],
             dst_ref=kv_ref.at[i, pl.ds(own_at - d * rows + skip, rows - skip), :],
             send_sem=kv_send.at[d - 1, i],
             recv_sem=kv_recv.at[d - 1, i],
-            device_id={"seq": seq + d},
+            device_id={"seq": target},
         )
 
     if far_rows < rows:
@@ -177,15 +184,15 @@
             kv_ref[:, pl.ds(own_at - d * rows + skip, rows - skip), :] = jnp.zeros(
                 (2, rows - skip, HD), jnp.bfloat16)
 
-    greeted = 3 + jnp.minimum(seq, reach) + jnp.minimum(cycle_size - 1 - seq, reach)
-    pl.semaphore_wait(barrier, greeted)
+    far_peer = core * jnp.minimum(1, (cycle_size - 1 - seq) // 3) + (1 - core) * jnp.minimum(1, seq // 3)
+    near_peers = jnp.minimum(1, (cycle_size - 1 - seq) // 2) + jnp.minimum(1, seq // 2)
+    pl.semaphore_wait(barrier, 3 + near_peers + far_peer)
 
     for i in range(2):
         own[i].wait()
-        for d in range(reach, 0, -1):
-            @pl.when(seq + d < cycle_size)
-            def _():
-                kv_copy(d, i).start()
+        pl.when(has_next)(lambda i=i: kv_copy(0, 2, i, seq + 2).start())
+        pl.when(sends_far)(lambda i=i: kv_copy(0, 3, i, seq + 3).start())
+        pl.when(core == 0)(lambda i=i: kv_copy(0, 1, i, partner).start())
 
     seg_load.wait()
     length = (reach + 1) * rows
@@ -201,26 +208,39 @@
 
     q_load.wait()
 
+    def relay(i):
+        @pl.when(has_last)
+        def _():
+            kv_copy(0, 2, i, partner).wait_recv()
+
+            @pl.when(core == 0)
+            def _():
+                kv_copy(2, 3, i, partner).start()
+
+            @pl.when(core == 1)
+            def _():
+                kv_copy(2, 1, i, partner).start()
+
     def arrivals(i):
-        for d in range(1, reach + 1):
-            @pl.when(seq - d >= 0)
-            def _():
-                kv_copy(d, i).wait_recv()
-
+        pl.when((core == 1) | has_last)(lambda: kv_copy(0, 1, i, partner).wait_recv())
+        pl.when(((core == 1) & has_last) | takes_far)(lambda: kv_copy(0, 3, i, partner).wait_recv())
+
+    relay(0)
+    relay(1)
     arrivals(0)
-    arrivals(1)
     factor = HD ** (-0.5) * math.log2(math.e)
 
-    def att_copy(r, c):
+    def att_copy(held, r, c, target):
         return pltpu.make_async_remote_copy(
-            src_ref=att_ref.at[0, c],
+            src_ref=att_ref.at[held, c],
             dst_ref=att_ref.at[r, c],
             send_sem=att_send.at[r - 1, c],
             recv_sem=att_recv.at[r - 1, c],
-            device_id={"head": peers[r]},
+            device_id={"head": peers[target]},
         )
 
     per_pair = group // PAIRS
+    probs, totals = [], []
     for h in range(group):
         q_h = q_ref[:, h * HD:(h + 1) * HD]
         scores = lax.dot_general(
@@ -228,20 +248,32 @@
         scores = jnp.where(allowed, scores, masked_score)
         row_max = jnp.max(scores, axis=1, keepdims=True)
         raw = jnp.exp2((scores - row_max) * factor)
-        total = jnp.sum(raw, axis=1, keepdims=True)
-        part = jnp.dot(raw.astype(jnp.bfloat16), kv_ref[1], preferred_element_type=jnp.float32)
+        totals.append(jnp.sum(raw, axis=1, keepdims=True))
+        probs.append(raw.astype(jnp.bfloat16))
+    arrivals(1)
+    for h in range(group):
+        part = jnp.dot(probs[h], kv_ref[1], preferred_element_type=jnp.float32)
         c, place = h // per_pair, h % per_pair
-        att_ref[0, c, :, place * HD:(place + 1) * HD] = (part / total).astype(jnp.bfloat16)
-        if place == per_pair - 1:
-            for r in (3, 1, 2):
-                att_copy(r, c).start()
-
-    order = [(0, 0), (0, 1)] + [(r, c) for c in range(PAIRS) for r in (1, 2, 3)]
+        att_ref[0, c, :, place * HD:(place + 1) * HD] = (part / totals[h]).astype(jnp.bfloat16)
+        if h == per_pair - 1:
+            att_copy(0, 1, 0, 1).start()
+    att_copy(0, 2, 1, 2).start()
+    att_copy(0, 1, 1, 1).start()
+    att_copy(0, 2, 0, 2).start()
+
+    order = [(0, 0), (0, 1), (1, 0), (2, 1), (1, 1), (2, 0), (3, 0), (3, 1)]
+    loaded = set()
     for step, (r, c) in enumerate(order):
-        if r:
-            att_copy(r, c).wait_recv()
-        if c == 0:
+        if step == 2:
+            att_copy(0, 1, 0, 1).wait_recv()
+            att_copy(1, 3, 0, 2).start()
+            att_copy(0, 2, 1, 2).wait_recv()
+            att_copy(2, 3, 1, 1).start()
+        elif step > 3:
+            att_copy(0, r, c, 1).wait_recv()
+        if r not in loaded:
             w_loads[r].wait()
+            loaded.add(r)
         piece = jnp.dot(
             att_ref[r, c], w_ref[r, c * pair_width:(c + 1) * pair_width, :],
             preferred_element_type=jnp.float32)
@@ -252,14 +284,13 @@
         else:
             out_ref[...] = (acc_ref[...] + piece).astype(jnp.bfloat16)
 
-    for d in range(1, reach + 1):
-        @pl.when(seq + d < cycle_size)
-        def _():
-            kv_copy(d, 0).wait_send()
-            kv_copy(d, 1).wait_send()
+    for i in range(2):
+        pl.when(has_next)(lambda i=i: kv_copy(0, 2, i, seq + 2).wait_send())
+        pl.when(sends_far | ((core == 0) & has_last))(lambda i=i: kv_copy(0, 3, i, partner).wait_send())
+        pl.when((core == 0) | has_last)(lambda i=i: kv_copy(0, 1, i, partner).wait_send())
     for r in range(1, 4):
         for c in range(PAIRS):
-            att_copy(r, c).wait_send()
+            att_copy(0, r, c, 1).wait_send()
 
 
 def fused(reach, queries, keys, values, segments, out_weight):
@@ -299,7 +330,7 @@
     row_count, width = queries.shape
     cycle_size = lax.axis_size("seq")
     reach = needed_reach(segments.shape[0], row_count, cycle_size)
-    fits = 1 <= reach <= MAX_REACH and lax.axis_size("head") == 4
+    fits = reach == REACH and cycle_size % 2 == 0 and lax.axis_size("head") == 4
     fits = fits and keys.shape[1] == HD and width % (PAIRS * HD) == 0
     if fits and row_count == HD and 4 * width == out_weight.shape[0]:
         return fused(reach, queries, keys, values, segments, out_weight)

time: 17.3 us -> 16.5 us (0.954)
  Pallas kernels: 16.4 us -> 15.5 us
    pallas_call x1, Pallas kernels: 16.4 us -> 15.5 us  [fused(): pl.pallas_call(functools.partial(fused_kernel, reach, far_rows, cycle_siz...]
where the time goes in v3:
time: 16.5 us; the launch traced here: 16.3 us
  Pallas kernels  15.5 us (94%)
  local copies, waits for them, and re-layouts  0.8 us (5%)
    pallas_call x1, Pallas kernels, fused(): pl.pallas_call(functools.partial(fused_kernel, reach, far_rows, cycle_siz...  15.5 us
    unnamed x1, local copies, waits for them, and re-layouts  0.8 us

profile of v3, /device:TPU:16, one launch (start us, length us, event | category | flops | bytes accessed | tf_op | source)
XLA Modules:
  0.0 16.3 jit_solution(6541128581632010651)
XLA Ops:
  0.0 15.5 %shard_map.55 = bf16[128,2048]{1,0:T(8,128)(2,1)S(1)} custom-call(bf16[128,512]{1,0:T(8,128)(2,1)} %q_hbm.1, bf16[128,128]{1,0:T(8,128)(2,1)} %k_hbm.1, bf16[128,128]{1,0:T(8,128)(2,1)} %v_hbm.1, s32[8,128]{1,0:T(8,128)} %bitcast.1, bf16[2048,2048]{1,0:T(8,128)(2,1)} %w_hbm.1), custom_call_target="tpu_custom_call" | custom-call | tf_op jit(solution)/shard_map/pallas_call | solution.py:305
  15.5 0.8 %copy.7 = bf16[128,2048]{1,0:T(8,128)(2,1)} copy(bf16[128,2048]{1,0:T(8,128)(2,1)S(1)} %shard_map.55) | data formatting | bytes 1048576

commit v4 on v3

--- a/solution.py
+++ b/solution.py
@@ -107,7 +107,7 @@
 
 SUBTILE = 16
 REACH = 3
-PAIRS = 2
+PAIRS = 4
 VMEM_GRANT = 32 * 2**20
 
 
@@ -251,26 +251,25 @@
         totals.append(jnp.sum(raw, axis=1, keepdims=True))
         probs.append(raw.astype(jnp.bfloat16))
     arrivals(1)
-    for h in range(group):
-        part = jnp.dot(probs[h], kv_ref[1], preferred_element_type=jnp.float32)
-        c, place = h // per_pair, h % per_pair
-        att_ref[0, c, :, place * HD:(place + 1) * HD] = (part / totals[h]).astype(jnp.bfloat16)
-        if h == per_pair - 1:
-            att_copy(0, 1, 0, 1).start()
-    att_copy(0, 2, 1, 2).start()
-    att_copy(0, 1, 1, 1).start()
-    att_copy(0, 2, 0, 2).start()
-
-    order = [(0, 0), (0, 1), (1, 0), (2, 1), (1, 1), (2, 0), (3, 0), (3, 1)]
+    half = PAIRS // 2
+    first_out = {1: tuple(range(half)), 2: tuple(range(half, PAIRS))}
+    turns = [(r, first_out[r][k]) for k in range(half) for r in (1, 2)]
+    for r, c in turns:
+        for place in range(per_pair):
+            h = c * per_pair + place
+            part = jnp.dot(probs[h], kv_ref[1], preferred_element_type=jnp.float32)
+            att_ref[0, c, :, place * HD:(place + 1) * HD] = (part / totals[h]).astype(jnp.bfloat16)
+        att_copy(0, r, c, r).start()
+    for r, c in turns:
+        att_copy(0, 3 - r, c, 3 - r).start()
+
+    order = [(0, c) for c in range(PAIRS)] + turns + [(3 - r, c) for r, c in turns] + [(3, c) for _, c in turns]
     loaded = set()
     for step, (r, c) in enumerate(order):
-        if step == 2:
-            att_copy(0, 1, 0, 1).wait_recv()
-            att_copy(1, 3, 0, 2).start()
-            att_copy(0, 2, 1, 2).wait_recv()
-            att_copy(2, 3, 1, 1).start()
-        elif step > 3:
+        if r:
             att_copy(0, r, c, 1).wait_recv()
+        if (r, c) in turns:
+            att_copy(r, 3, c, 3 - r).start()
         if r not in loaded:
             w_loads[r].wait()
             loaded.add(r)

time: 16.5 us -> 16.1 us (0.976)
  Pallas kernels: 15.5 us -> 15.2 us
    pallas_call x1, Pallas kernels: 15.5 us -> 15.2 us  [fused(): pl.pallas_call(functools.partial(fused_kernel, reach, far_rows, cycle_siz...]
where the time goes in v4:
time: 16.1 us; the launch traced here: 16 us
  Pallas kernels  15.2 us (94%)
  local copies, waits for them, and re-layouts  0.8 us (5%)
    pallas_call x1, Pallas kernels, fused(): pl.pallas_call(functools.partial(fused_kernel, reach, far_rows, cycle_siz...  15.2 us
    unnamed x1, local copies, waits for them, and re-layouts  0.8 us

profile of v4, /device:TPU:16, one launch (start us, length us, event | category | flops | bytes accessed | tf_op | source)
XLA Modules:
  0.0 16.0 jit_solution(3496171550164926069)
XLA Ops:
  0.0 15.2 %shard_map.55 = bf16[128,2048]{1,0:T(8,128)(2,1)S(1)} custom-call(bf16[128,512]{1,0:T(8,128)(2,1)} %q_hbm.1, bf16[128,128]{1,0:T(8,128)(2,1)} %k_hbm.1, bf16[128,128]{1,0:T(8,128)(2,1)} %v_hbm.1, s32[8,128]{1,0:T(8,128)} %bitcast.1, bf16[2048,2048]{1,0:T(8,128)(2,1)} %w_hbm.1), custom_call_target="tpu_custom_call" | custom-call | tf_op jit(solution)/shard_map/pallas_call | solution.py:304
  15.2 0.8 %copy.7 = bf16[128,2048]{1,0:T(8,128)(2,1)} copy(bf16[128,2048]{1,0:T(8,128)(2,1)S(1)} %shard_map.55) | data formatting | bytes 1048576
